TPU v7x, 32 devices: a whole 2x2x4 slice. The times are simulated.
32 devices in a mesh: row: 4 (over y, core), col: 8 (over z, x).
Axes of the slice: x: 2, y: 2, z: 4, core: 2. Of those that a mesh axis runs over, the one named last changes fastest.
Arguments:
- obs_cell: int32 [32, 16, 32, 128], P(('row', 'col')), may hold values from 0 to 8388607, as said below
- obs_value: bfloat16 [32, 16, 32, 128], P(('row', 'col')), may hold values from -6 to 6
- obs_weight: bfloat16 [32, 16, 32, 128], P(('row', 'col')), may hold values from 0.5 to 2
- obs_count: int32 [32, 16, 32], P(('row', 'col')), may hold values from 0 to 128, as said below
- kappa_field: float32 [2048, 4096], P('row', 'col'), may hold values from 0.2 to 6
Outputs:
- solution_field: float32 [2048, 4096], P('row', 'col')
- residual: float32 [2048, 4096], P('row', 'col')
Inputs may be any that keep to these rules, and one draw needn't show every extreme that they name: `obs_cell`: block (s, t, d) holds observations for tile t of device d, where device d is number d // 8 along row and d % (8) along col, and tile t is number t // 4 among the device's tiles along rows and t % (4) along columns, each tile 128 by 128 cells; every slot of the block, padding included, names a cell of that tile as row * 4096 + column. Slots at positions obs_count and beyond are padding. For one owner device, chosen afresh in each draw, every block from every source and tile is full.
All inputs are finite; a program needn't handle non-finite values.
Results may differ from a plain program's by a relative error of at most 0.0029.
Values may be sent and summed in bfloat16 or wider, within the bound.
A program may use at most 64 MiB of HBM per device.

v0:
```python
from functools import partial

import jax
import jax.numpy as jnp
from jax import lax
from jax.sharding import PartitionSpec as P

TILE = 128
ITERS = 3


smooth_weight = 0.05


def extended(block, sides, width):
    for axis, dim in sides:
        count = lax.axis_size(axis)
        forward = [(i, i + 1) for i in range(count - 1)]
        backward = [(target, source) for source, target in forward]
        low = lax.ppermute(
            lax.slice_in_dim(block, block.shape[dim] - width, None, axis=dim), axis, forward
        )
        high = lax.ppermute(lax.slice_in_dim(block, 0, width, axis=dim), axis, backward)
        block = jnp.concatenate([low, block, high], axis=dim)
    return block


def stencil_step(padded, kappa_field):
    center = padded[1:-1, 1:-1]
    beside = padded[2:, 1:-1] + padded[:-2, 1:-1]
    beside = beside + padded[1:-1, 2:] + padded[1:-1, :-2]
    return (4.0 + kappa_field) * center - beside


def bin_tile(members, cols_all):
    cell_ids, obs_vals, obs_wts, is_live = members
    local_row = cell_ids // cols_all % TILE
    local_col = cell_ids % cols_all % TILE
    offsets = jnp.arange(TILE, dtype=jnp.int32)
    row_onehot = (local_row[:, None] == offsets[None, :]).astype(jnp.bfloat16)
    col_onehot = (local_col[:, None] == offsets[None, :]).astype(jnp.bfloat16)
    zero_fill = jnp.zeros_like(obs_wts)
    masked_weight = jnp.where(is_live, obs_wts, zero_fill)
    product = (obs_wts.astype(jnp.float32) * obs_vals.astype(jnp.float32)).astype(jnp.bfloat16)
    masked_resp = jnp.where(is_live, product, zero_fill)
    stacked = jnp.concatenate(
        [col_onehot * masked_weight[:, None], col_onehot * masked_resp[:, None]], axis=1
    )
    return lax.dot_general(
        row_onehot, stacked, (((0,), (0,)), ((), ())), preferred_element_type=jnp.float32
    )


def per_device(obs_cell, obs_value, obs_weight, obs_count, kappa_field):
    rows_dev, cols_dev = kappa_field.shape
    cols_all = cols_dev * lax.axis_size("col")
    tiles_dev = obs_cell.shape[1]
    block_rows = obs_cell.shape[3]
    got_cells, got_counts = (
        lax.all_to_all(obs_cell, ("row", "col"), split_axis=2, concat_axis=2, tiled=True),
        lax.all_to_all(obs_count, ("row", "col"), split_axis=2, concat_axis=2, tiled=True),
    )
    got_values, got_weights = (
        lax.all_to_all(obs_value, ("row", "col"), split_axis=2, concat_axis=2, tiled=True),
        lax.all_to_all(obs_weight, ("row", "col"), split_axis=2, concat_axis=2, tiled=True),
    )
    flat_rows = obs_cell.shape[2] * block_rows
    positions = jnp.arange(block_rows, dtype=jnp.int32)
    is_live = (positions[None, None, :] < got_counts.reshape(tiles_dev, -1)[:, :, None]).reshape(
        tiles_dev, flat_rows
    )
    members = (
        got_cells.reshape(tiles_dev, flat_rows),
        got_values.reshape(tiles_dev, flat_rows),
        got_weights.reshape(tiles_dev, flat_rows),
        is_live,
    )
    binned = lax.map(partial(bin_tile, cols_all=cols_all), members)
    tile_rows = rows_dev // TILE
    tile_cols = cols_dev // TILE
    binned = (
        binned.reshape(tile_rows, tile_cols, TILE, 2, TILE)
        .transpose(3, 0, 2, 1, 4)
        .reshape(2, rows_dev, cols_dev)
    )
    weight_field = binned[0]
    response = binned[1]

    def operate(field):
        first = extended(field, (("row", 0), ("col", 1)), 1)
        inner = stencil_step(first, kappa_field)
        second = extended(inner, (("row", 0), ("col", 1)), 1)
        return weight_field * field + smooth_weight * stencil_step(second, kappa_field)

    solution_field = jnp.zeros_like(response)
    residual = response

    def two_products(current, image):
        return lax.psum((jnp.sum(current * current), jnp.sum(current * image)), ("row", "col"))

    image = operate(residual)
    norm_now, curvature = two_products(residual, image)
    alpha = norm_now / curvature
    direction, along = (residual, image)
    for step in range(ITERS):
        solution_field = solution_field + alpha * direction
        residual = residual - alpha * along
        if step + 1 < ITERS:
            image = operate(residual)
            norm_next, curvature = two_products(residual, image)
            ratio = norm_next / norm_now
            alpha = norm_next / (curvature - ratio * norm_next / alpha)
            direction = residual + ratio * direction
            along = image + ratio * along
            norm_now = norm_next
    return (solution_field, residual)


def solution(mesh):
    placed = (
        P(("row", "col"), None, None, None),
        P(("row", "col"), None, None, None),
        P(("row", "col"), None, None, None),
        P(("row", "col"), None, None),
        P("row", "col"),
    )
    return jax.shard_map(
        per_device,
        mesh=mesh,
        in_specs=placed,
        out_specs=(P("row", "col"), P("row", "col")),
        check_vma=False,
    )
```

profile of v0, /device:TPU:0, one launch (start us, length us, event | category | flops | bytes accessed | tf_op | source)
XLA Modules:
  0.0 424.5 jit_solution(13311932666679719868)
XLA Ops:
  2.0 7.3 %all-to-all-start.1 = ((s32[1,16,32]{1,0,2:T(1,128)}), s32[1,16,32]{1,0,2:T(1,128)S(1)}, u32[]{:S(2)}, u32[]{:S(2)}) async-start(s32[1,16,32]{1,0,2:T(1,128)} %copy.16), calls=%async_computation.1 | async-start | bytes 32768 | tf_op jit(solution)/shard_map/all_to_all | solution.py:61
  9.3 1.6 copy.20
  11.0 5.5 %all-to-all-done.1 = s32[1,16,32]{1,0,2:T(1,128)S(1)} async-done(((s32[1,16,32]{1,0,2:T(1,128)}), s32[1,16,32]{1,0,2:T(1,128)S(1)}, u32[]{:S(2)}, u32[]{:S(2)}) %all-to-all-start.1) | async-done | bytes 2080 | tf_op jit(solution)/shard_map/all_to_all | solution.py:61
  16.4 2.6 all-to-all-start.3
  20.6 1.8 copy.14
  22.5 4.3 %all-to-all-done.3 = bf16[1,16,32,128]{3,1,0,2:T(8,128)(2,1)S(1)} async-done(((bf16[1,16,32,128]{3,1,0,2:T(8,128)(2,1)}), bf16[1,16,32,128]{3,1,0,2:T(8,128)(2,1)S(1)}, u32[]{:S(2)}, u32[]{:S(2)}) %all-to-all-start.3) | async-done | bytes 131104 | tf_op jit(solution)/shard_map/all_to_all | solution.py:64
  26.8 2.6 all-to-all-start.2
  30.3 6.8 %all-to-all-done.2 = bf16[1,16,32,128]{3,1,0,2:T(8,128)(2,1)S(1)} async-done(((bf16[1,16,32,128]{3,1,0,2:T(8,128)(2,1)}), bf16[1,16,32,128]{3,1,0,2:T(8,128)(2,1)S(1)}, u32[]{:S(2)}, u32[]{:S(2)}) %all-to-all-start.2) | async-done | bytes 131104 | tf_op jit(solution)/shard_map/all_to_all | solution.py:65
  37.2 2.6 all-to-all-start
  40.6 9.7 %all-to-all-done = s32[1,16,32,128]{3,1,0,2:T(8,128)S(1)} async-done(((s32[1,16,32,128]{3,1,0,2:T(8,128)}), s32[1,16,32,128]{3,1,0,2:T(8,128)S(1)}, u32[]{:S(2)}, u32[]{:S(2)}) %all-to-all-start) | async-done | bytes 262176 | tf_op jit(solution)/shard_map/all_to_all | solution.py:60
  50.5 83.1 %while.13 = (s32[]{:T(128)}, f32[16,128,256]{2,1,0:T(8,128)S(1)}, s32[16,4096]{1,0:T(8,128)S(1)}, pred[16,4096]{1,0:T(8,128)(4,1)}, bf16[16,4096]{1,0:T(8,128)(2,1)}, /*index=5*/bf16[16,4096]{1,0:T(8,128)(2,1)S(1)}, s32[]{:T(128)}) while((s32[]{:T(128)}, f32[16,128,256]{2,1,0:T(8,128)S(1)}, s32[16,4096]{1,0:T(8,128)S(1)}, ...), condition=%wide.region_1.2_spmd, body=%wide.region_0.1_spmd.sunk | while | flops 274919424 | bytes 4550757 | solution.py:78
  52.3 1.9 fusion.62
  57.5 1.9 fusion.62
  62.7 1.9 fusion.62
  67.9 1.9 fusion.62
  73.1 1.9 fusion.62
  78.3 1.9 fusion.62
  83.5 1.9 fusion.62
  88.7 1.9 fusion.62
  93.9 1.9 fusion.62
  99.0 1.9 fusion.62
  104.2 1.9 fusion.62
  109.4 1.9 fusion.62
  114.6 1.9 fusion.62
  119.8 1.9 fusion.62
  125.0 1.9 fusion.62
  130.2 1.9 fusion.62
  134.9 2.3 reshape.137
  139.8 2.1 collective-permute-start.1
  143.3 2.0 collective-permute-done
  146.7 4.6 %collective-permute-start.3 = (f32[514,1]{1,0:T(8,128)S(1)}, f32[514,1]{1,0:T(8,128)S(1)}, u32[]{:S(2)}, u32[]{:S(2)}) collective-permute-start(f32[514,1]{1,0:T(8,128)S(1)} %get-tuple-element.158), channel_id=1, source_target_pairs={{0,1},{1,2},{2,3},{3,4},{4,5},{5,6},{6,7},{8,9},{9,10},{10,11},{11... | collective-permute-start | bytes 6176 | tf_op jit(solution)/shard_map/ppermute | solution.py:20
  151.2 3.9 collective-permute-done.2
  155.2 6.6 %collective-permute-done.3 = f32[514,1]{1,0:T(8,128)S(1)} collective-permute-done((f32[514,1]{1,0:T(8,128)S(1)}, f32[514,1]{1,0:T(8,128)S(1)}, u32[]{:S(2)}, u32[]{:S(2)}) %collective-permute-start.3) | collective-permute-done | bytes 2088 | tf_op jit(solution)/shard_map/ppermute | solution.py:20
  162.5 2.2 collective-permute-start.5
  166.1 1.7 collective-permute-done.4
  169.3 4.8 %collective-permute-start.7 = (f32[514,1]{1,0:T(8,128)S(1)}, f32[514,1]{1,0:T(8,128)S(1)}, u32[]{:S(2)}, u32[]{:S(2)}) collective-permute-start(f32[514,1]{1,0:T(8,128)S(1)} %get-tuple-element.156), channel_id=1, source_target_pairs={{0,1},{1,2},{2,3},{3,4},{4,5},{5,6},{6,7},{8,9},{9,10},{10,11},{11... | collective-permute-start | bytes 6176 | tf_op jit(solution)/shard_map/ppermute | solution.py:20
  174.1 4.1 collective-permute-done.6
  178.2 7.2 %collective-permute-done.7 = f32[514,1]{1,0:T(8,128)S(1)} collective-permute-done((f32[514,1]{1,0:T(8,128)S(1)}, f32[514,1]{1,0:T(8,128)S(1)}, u32[]{:S(2)}, u32[]{:S(2)}) %collective-permute-start.7) | collective-permute-done | bytes 2088 | tf_op jit(solution)/shard_map/ppermute | solution.py:20
  185.4 2.6 multiply_reduce_fusion.4
  188.0 39.1 %all-reduce.2 = (f32[]{:T(128)}, f32[]{:T(128)}) all-reduce(f32[]{:T(128)} %get-tuple-element.144, f32[]{:T(128)} %get-tuple-element.134), channel_id=1, replica_groups=mesh['row'=4,'col'=8] {'row','col'}, use_global_device_ids=true, to_apply=%region_3.4 | all-reduce | flops 2 | bytes 16 | tf_op jit(solution)/shard_map/psum | solution.py:99
  232.4 4.5 %collective-permute-done.8 = f32[1,512]{1,0:T(1,128)S(1)} collective-permute-done((f32[1,512]{1,0:T(1,128)S(1)}, f32[1,512]{1,0:T(1,128)S(1)}, u32[]{:S(2)}, u32[]{:S(2)}) %collective-permute-start.8) | collective-permute-done | bytes 2080 | tf_op jit(solution)/shard_map/ppermute | solution.py:23
  238.4 4.7 %collective-permute-start.11 = (f32[514,1]{1,0:T(8,128)S(1)}, f32[514,1]{1,0:T(8,128)S(1)}, u32[]{:S(2)}, u32[]{:S(2)}) collective-permute-start(f32[514,1]{1,0:T(8,128)S(1)} %get-tuple-element.154), channel_id=1, source_target_pairs={{0,1},{1,2},{2,3},{3,4},{4,5},{5,6},{6,7},{8,9},{9,10},{10,11},{11... | collective-permute-start | bytes 6176 | tf_op jit(solution)/shard_map/ppermute | solution.py:20
  243.1 3.7 collective-permute-done.10
  246.8 7.3 %collective-permute-done.11 = f32[514,1]{1,0:T(8,128)S(1)} collective-permute-done((f32[514,1]{1,0:T(8,128)S(1)}, f32[514,1]{1,0:T(8,128)S(1)}, u32[]{:S(2)}, u32[]{:S(2)}) %collective-permute-start.11) | collective-permute-done | bytes 2088 | tf_op jit(solution)/shard_map/ppermute | solution.py:20
  254.9 2.2 collective-permute-start.13
  258.4 1.7 collective-permute-done.12
  261.6 5.0 %collective-permute-start.15 = (f32[514,1]{1,0:T(8,128)S(1)}, f32[514,1]{1,0:T(8,128)S(1)}, u32[]{:S(2)}, u32[]{:S(2)}) collective-permute-start(f32[514,1]{1,0:T(8,128)S(1)} %get-tuple-element.152), channel_id=1, source_target_pairs={{0,1},{1,2},{2,3},{3,4},{4,5},{5,6},{6,7},{8,9},{9,10},{10,11},{11... | collective-permute-start | bytes 6176 | tf_op jit(solution)/shard_map/ppermute | solution.py:20
  266.6 3.9 collective-permute-done.14
  270.6 7.2 %collective-permute-done.15 = f32[514,1]{1,0:T(8,128)S(1)} collective-permute-done((f32[514,1]{1,0:T(8,128)S(1)}, f32[514,1]{1,0:T(8,128)S(1)}, u32[]{:S(2)}, u32[]{:S(2)}) %collective-permute-start.15) | collective-permute-done | bytes 2088 | tf_op jit(solution)/shard_map/ppermute | solution.py:20
  277.8 2.6 multiply_reduce_fusion.2
  280.4 40.2 %all-reduce.1 = (f32[]{:T(128)}, f32[]{:T(128)}) all-reduce(f32[]{:T(128)} %get-tuple-element.113, f32[]{:T(128)} %get-tuple-element.112), channel_id=1, replica_groups=mesh['row'=4,'col'=8] {'row','col'}, use_global_device_ids=true, to_apply=%region_7.8 | all-reduce | flops 2 | bytes 16 | tf_op jit(solution)/shard_map/psum | solution.py:99
  325.0 1.9 multiply_subtract_fusion.1
  329.5 4.5 %collective-permute-done.16 = f32[1,512]{1,0:T(1,128)S(1)} collective-permute-done((f32[1,512]{1,0:T(1,128)S(1)}, f32[1,512]{1,0:T(1,128)S(1)}, u32[]{:S(2)}, u32[]{:S(2)}) %collective-permute-start.16) | collective-permute-done | bytes 2080 | tf_op jit(solution)/shard_map/ppermute | solution.py:23
  335.5 4.7 %collective-permute-start.19 = (f32[514,1]{1,0:T(8,128)S(1)}, f32[514,1]{1,0:T(8,128)S(1)}, u32[]{:S(2)}, u32[]{:S(2)}) collective-permute-start(f32[514,1]{1,0:T(8,128)S(1)} %get-tuple-element.150), channel_id=1, source_target_pairs={{0,1},{1,2},{2,3},{3,4},{4,5},{5,6},{6,7},{8,9},{9,10},{10,11},{11... | collective-permute-start | bytes 6176 | tf_op jit(solution)/shard_map/ppermute | solution.py:20
  340.2 3.7 collective-permute-done.18
  343.9 7.3 %collective-permute-done.19 = f32[514,1]{1,0:T(8,128)S(1)} collective-permute-done((f32[514,1]{1,0:T(8,128)S(1)}, f32[514,1]{1,0:T(8,128)S(1)}, u32[]{:S(2)}, u32[]{:S(2)}) %collective-permute-start.19) | collective-permute-done | bytes 2088 | tf_op jit(solution)/shard_map/ppermute | solution.py:20
  352.0 2.2 collective-permute-start.21
  355.5 1.7 collective-permute-done.20
  358.7 4.8 %collective-permute-start.23 = (f32[514,1]{1,0:T(8,128)S(1)}, f32[514,1]{1,0:T(8,128)S(1)}, u32[]{:S(2)}, u32[]{:S(2)}) collective-permute-start(f32[514,1]{1,0:T(8,128)S(1)} %get-tuple-element.148), channel_id=1, source_target_pairs={{0,1},{1,2},{2,3},{3,4},{4,5},{5,6},{6,7},{8,9},{9,10},{10,11},{11... | collective-permute-start | bytes 6176 | tf_op jit(solution)/shard_map/ppermute | solution.py:20
  363.5 4.1 collective-permute-done.22
  367.6 7.2 %collective-permute-done.23 = f32[514,1]{1,0:T(8,128)S(1)} collective-permute-done((f32[514,1]{1,0:T(8,128)S(1)}, f32[514,1]{1,0:T(8,128)S(1)}, u32[]{:S(2)}, u32[]{:S(2)}) %collective-permute-start.23) | collective-permute-done | bytes 2088 | tf_op jit(solution)/shard_map/ppermute | solution.py:20
  374.9 2.6 multiply_reduce_fusion
  377.5 39.0 %all-reduce = (f32[]{:T(128)}, f32[]{:T(128)}) all-reduce(f32[]{:T(128)} %get-tuple-element.111, f32[]{:T(128)} %get-tuple-element.110), channel_id=1, replica_groups=mesh['row'=4,'col'=8] {'row','col'}, use_global_device_ids=true, to_apply=%region_11.12 | all-reduce | flops 2 | bytes 16 | tf_op jit(solution)/shard_map/psum | solution.py:99
  420.3 4.3 %multiply_subtract_fusion = (f32[512,512]{1,0:T(8,128)}, f32[512,512]{1,0:T(8,128)}) fusion(f32[512,512]{1,0:T(8,128)S(1)} %multiply_subtract_fusion.1, f32[512,512]{1,0:T(8,128)} %get-tuple-element.132, f32[]{:T(128)S(6)} %div.37, f32[]{:T(128)S(6)} %div.39, f32[512,512]{1,0:T(8,128)} %get-tuple-element.133, f32[512,512]{1,0:T(8,128)} %get-tuple-element.135, ...), kind=kLoop, calls=%fused_computation.118 | loop fusion | flops 3932160 | bytes 8388628 | tf_op jit(solution)/shard_map/sub | solution.py:107
  (159 shorter events, 83.1 us)
Async XLA Ops:
  2.0 14.4 %all-to-all-start.1 = ((s32[1,16,32]{1,0,2:T(1,128)}), s32[1,16,32]{1,0,2:T(1,128)S(1)}, u32[]{:S(2)}, u32[]{:S(2)}) async-start(s32[1,16,32]{1,0,2:T(1,128)} %copy.16), calls=%async_computation.1 | async-start | bytes 32768 | tf_op jit(solution)/shard_map/all_to_all | solution.py:61
  16.4 10.4 %all-to-all-start.3 = ((bf16[1,16,32,128]{3,1,0,2:T(8,128)(2,1)}), bf16[1,16,32,128]{3,1,0,2:T(8,128)(2,1)S(1)}, u32[]{:S(2)}, u32[]{:S(2)}) async-start(bf16[1,16,32,128]{3,1,0,2:T(8,128)(2,1)} %copy.20), calls=%async_computation.3 | async-start | bytes 262144 | tf_op jit(solution)/shard_map/all_to_all | solution.py:64
  26.8 10.4 %all-to-all-start.2 = ((bf16[1,16,32,128]{3,1,0,2:T(8,128)(2,1)}), bf16[1,16,32,128]{3,1,0,2:T(8,128)(2,1)S(1)}, u32[]{:S(2)}, u32[]{:S(2)}) async-start(bf16[1,16,32,128]{3,1,0,2:T(8,128)(2,1)} %copy.18), calls=%async_computation.2 | async-start | bytes 262144 | tf_op jit(solution)/shard_map/all_to_all | solution.py:65
  37.2 13.0 %all-to-all-start = ((s32[1,16,32,128]{3,1,0,2:T(8,128)}), s32[1,16,32,128]{3,1,0,2:T(8,128)S(1)}, u32[]{:S(2)}, u32[]{:S(2)}) async-start(s32[1,16,32,128]{3,1,0,2:T(8,128)} %copy.14), calls=%async_computation | async-start | bytes 524288 | tf_op jit(solution)/shard_map/all_to_all | solution.py:60
  133.6 1.3 copy-start.5
  139.7 45.7 %copy-start.2 = (f32[1,4,128,4,128]{4,3,2,1,0:T(4,128)}, f32[1,4,128,4,128]{4,3,2,1,0:T(4,128)S(1)}, u32[]{:S(2)}) copy-start(f32[1,4,128,4,128]{4,3,2,1,0:T(4,128)S(1)} %get-tuple-element.145) | copy-start | bytes 3145732
  139.8 88.6 %copy-start.1 = (f32[1,4,128,4,128]{4,3,2,1,0:T(4,128)}, f32[1,4,128,4,128]{4,3,2,1,0:T(4,128)S(1)}, u32[]{:S(2)}) copy-start(f32[1,4,128,4,128]{4,3,2,1,0:T(4,128)S(1)} %get-tuple-element.146) | copy-start | bytes 3145732
  139.8 22.0 %copy-start = (f32[512,512]{1,0:T(8,128)S(1)}, f32[512,512]{1,0:T(8,128)}, u32[]{:S(2)}) copy-start(f32[512,512]{1,0:T(8,128)} %param.11) | copy-start | bytes 3145732
  139.8 3.4 collective-permute-start.1
  141.9 3.3 collective-permute-start
  145.4 9.8 %collective-permute-start.2 = (f32[514,1]{1,0:T(8,128)S(1)}, f32[514,1]{1,0:T(8,128)S(1)}, u32[]{:S(2)}, u32[]{:S(2)}) collective-permute-start(f32[514,1]{1,0:T(8,128)S(1)} %get-tuple-element.157), channel_id=1, source_target_pairs={{1,0},{2,1},{3,2},{4,3},{5,4},{6,5},{7,6},{9,8},{10,9},{11,10},{12... | collective-permute-start | bytes 6176 | tf_op jit(solution)/shard_map/ppermute | solution.py:23
  146.7 15.1 %collective-permute-start.3 = (f32[514,1]{1,0:T(8,128)S(1)}, f32[514,1]{1,0:T(8,128)S(1)}, u32[]{:S(2)}, u32[]{:S(2)}) collective-permute-start(f32[514,1]{1,0:T(8,128)S(1)} %get-tuple-element.158), channel_id=1, source_target_pairs={{0,1},{1,2},{2,3},{3,4},{4,5},{5,6},{6,7},{8,9},{9,10},{10,11},{11... | collective-permute-start | bytes 6176 | tf_op jit(solution)/shard_map/ppermute | solution.py:20
  162.5 3.5 collective-permute-start.5
  164.7 3.1 collective-permute-start.4
  168.0 10.3 %collective-permute-start.6 = (f32[514,1]{1,0:T(8,128)S(1)}, f32[514,1]{1,0:T(8,128)S(1)}, u32[]{:S(2)}, u32[]{:S(2)}) collective-permute-start(f32[514,1]{1,0:T(8,128)S(1)} %get-tuple-element.155), channel_id=1, source_target_pairs={{1,0},{2,1},{3,2},{4,3},{5,4},{6,5},{7,6},{9,8},{10,9},{11,10},{12... | collective-permute-start | bytes 6176 | tf_op jit(solution)/shard_map/ppermute | solution.py:23
  169.3 16.2 %collective-permute-start.7 = (f32[514,1]{1,0:T(8,128)S(1)}, f32[514,1]{1,0:T(8,128)S(1)}, u32[]{:S(2)}, u32[]{:S(2)}) collective-permute-start(f32[514,1]{1,0:T(8,128)S(1)} %get-tuple-element.156), channel_id=1, source_target_pairs={{0,1},{1,2},{2,3},{3,4},{4,5},{5,6},{6,7},{8,9},{9,10},{10,11},{11... | collective-permute-start | bytes 6176 | tf_op jit(solution)/shard_map/ppermute | solution.py:20
  229.8 2.6 collective-permute-start.9
  231.1 5.8 %collective-permute-start.8 = (f32[1,512]{1,0:T(1,128)S(1)}, f32[1,512]{1,0:T(1,128)S(1)}, u32[]{:S(2)}, u32[]{:S(2)}) collective-permute-start(f32[1,512]{1,0:T(1,128)S(1)} %get-tuple-element.168), channel_id=1, source_target_pairs={{8,0},{16,8},{24,16},{9,1},{17,9},{25,17},{10,2},{18,10},{26,18},{... | collective-permute-start | bytes 6152 | tf_op jit(solution)/shard_map/ppermute | solution.py:23
  237.1 9.7 %collective-permute-start.10 = (f32[514,1]{1,0:T(8,128)S(1)}, f32[514,1]{1,0:T(8,128)S(1)}, u32[]{:S(2)}, u32[]{:S(2)}) collective-permute-start(f32[514,1]{1,0:T(8,128)S(1)} %get-tuple-element.153), channel_id=1, source_target_pairs={{1,0},{2,1},{3,2},{4,3},{5,4},{6,5},{7,6},{9,8},{10,9},{11,10},{12... | collective-permute-start | bytes 6176 | tf_op jit(solution)/shard_map/ppermute | solution.py:23
  238.4 39.4 %copy-start.3 = (f32[1,4,128,4,128]{4,3,2,1,0:T(4,128)S(1)}, f32[1,4,128,4,128]{4,3,2,1,0:T(4,128)}, u32[]{:S(2)}) copy-start(f32[1,4,128,4,128]{4,3,2,1,0:T(4,128)} %copy-done.2) | copy-start | bytes 3145732
  238.4 15.7 %collective-permute-start.11 = (f32[514,1]{1,0:T(8,128)S(1)}, f32[514,1]{1,0:T(8,128)S(1)}, u32[]{:S(2)}, u32[]{:S(2)}) collective-permute-start(f32[514,1]{1,0:T(8,128)S(1)} %get-tuple-element.154), channel_id=1, source_target_pairs={{0,1},{1,2},{2,3},{3,4},{4,5},{5,6},{6,7},{8,9},{9,10},{10,11},{11... | collective-permute-start | bytes 6176 | tf_op jit(solution)/shard_map/ppermute | solution.py:20
  254.9 3.5 collective-permute-start.13
  257.1 3.1 collective-permute-start.12
  260.3 10.3 %collective-permute-start.14 = (f32[514,1]{1,0:T(8,128)S(1)}, f32[514,1]{1,0:T(8,128)S(1)}, u32[]{:S(2)}, u32[]{:S(2)}) collective-permute-start(f32[514,1]{1,0:T(8,128)S(1)} %get-tuple-element.151), channel_id=1, source_target_pairs={{1,0},{2,1},{3,2},{4,3},{5,4},{6,5},{7,6},{9,8},{10,9},{11,10},{12... | collective-permute-start | bytes 6176 | tf_op jit(solution)/shard_map/ppermute | solution.py:23
  261.6 16.2 %collective-permute-start.15 = (f32[514,1]{1,0:T(8,128)S(1)}, f32[514,1]{1,0:T(8,128)S(1)}, u32[]{:S(2)}, u32[]{:S(2)}) collective-permute-start(f32[514,1]{1,0:T(8,128)S(1)} %get-tuple-element.152), channel_id=1, source_target_pairs={{0,1},{1,2},{2,3},{3,4},{4,5},{5,6},{6,7},{8,9},{9,10},{10,11},{11... | collective-permute-start | bytes 6176 | tf_op jit(solution)/shard_map/ppermute | solution.py:20
  326.9 2.6 collective-permute-start.17
  328.2 5.8 %collective-permute-start.16 = (f32[1,512]{1,0:T(1,128)S(1)}, f32[1,512]{1,0:T(1,128)S(1)}, u32[]{:S(2)}, u32[]{:S(2)}) collective-permute-start(f32[1,512]{1,0:T(1,128)S(1)} %get-tuple-element.164), channel_id=1, source_target_pairs={{8,0},{16,8},{24,16},{9,1},{17,9},{25,17},{10,2},{18,10},{26,18},{... | collective-permute-start | bytes 6152 | tf_op jit(solution)/shard_map/ppermute | solution.py:23
  334.2 9.7 %collective-permute-start.18 = (f32[514,1]{1,0:T(8,128)S(1)}, f32[514,1]{1,0:T(8,128)S(1)}, u32[]{:S(2)}, u32[]{:S(2)}) collective-permute-start(f32[514,1]{1,0:T(8,128)S(1)} %get-tuple-element.149), channel_id=1, source_target_pairs={{1,0},{2,1},{3,2},{4,3},{5,4},{6,5},{7,6},{9,8},{10,9},{11,10},{12... | collective-permute-start | bytes 6176 | tf_op jit(solution)/shard_map/ppermute | solution.py:23
  335.5 39.4 %copy-start.4 = (f32[1,4,128,4,128]{4,3,2,1,0:T(4,128)S(1)}, f32[1,4,128,4,128]{4,3,2,1,0:T(4,128)}, u32[]{:S(2)}) copy-start(f32[1,4,128,4,128]{4,3,2,1,0:T(4,128)} %copy-done.2) | copy-start | bytes 3145732
  335.5 15.7 %collective-permute-start.19 = (f32[514,1]{1,0:T(8,128)S(1)}, f32[514,1]{1,0:T(8,128)S(1)}, u32[]{:S(2)}, u32[]{:S(2)}) collective-permute-start(f32[514,1]{1,0:T(8,128)S(1)} %get-tuple-element.150), channel_id=1, source_target_pairs={{0,1},{1,2},{2,3},{3,4},{4,5},{5,6},{6,7},{8,9},{9,10},{10,11},{11... | collective-permute-start | bytes 6176 | tf_op jit(solution)/shard_map/ppermute | solution.py:20
  352.0 3.5 collective-permute-start.21
  354.2 3.1 collective-permute-start.20
  357.4 10.3 %collective-permute-start.22 = (f32[514,1]{1,0:T(8,128)S(1)}, f32[514,1]{1,0:T(8,128)S(1)}, u32[]{:S(2)}, u32[]{:S(2)}) collective-permute-start(f32[514,1]{1,0:T(8,128)S(1)} %get-tuple-element.147), channel_id=1, source_target_pairs={{1,0},{2,1},{3,2},{4,3},{5,4},{6,5},{7,6},{9,8},{10,9},{11,10},{12... | collective-permute-start | bytes 6176 | tf_op jit(solution)/shard_map/ppermute | solution.py:23
  358.7 16.2 %collective-permute-start.23 = (f32[514,1]{1,0:T(8,128)S(1)}, f32[514,1]{1,0:T(8,128)S(1)}, u32[]{:S(2)}, u32[]{:S(2)}) collective-permute-start(f32[514,1]{1,0:T(8,128)S(1)} %get-tuple-element.148), channel_id=1, source_target_pairs={{0,1},{1,2},{2,3},{3,4},{4,5},{5,6},{6,7},{8,9},{9,10},{10,11},{11... | collective-permute-start | bytes 6176 | tf_op jit(solution)/shard_map/ppermute | solution.py:20
where the time goes:
time: 428 us; the launch traced here: 425 us
  blocking collectives  118 us (28%)
  waiting for transfers between devices  109 us (25%)
  starting transfers between devices  70.5 us (16%)
  other arithmetic  66.7 us (16%)
  local copies, waits for them, and re-layouts  26.2 us (6%)
  matrix products  22.6 us (5%)
  between operations  10.6 us (2%)
    psum x3, blocking collectives, two_products(): lax.psum((jnp.sum(current * current), jnp.sum(current * image)), ('row',...  118 us
    ppermute x12, waiting for transfers between devices, extended(): lax.ppermute(lax.slice_in_dim(block, block.shape[dim] - width, None, axis...  43 us
    ppermute x12, starting transfers between devices, extended(): lax.ppermute(lax.slice_in_dim(block, block.shape[dim] - width, None, axis...  40 us
    ppermute x12, waiting for transfers between devices, extended(): lax.ppermute(lax.slice_in_dim(block, 0, width, axis=dim), axis, backward)  39.6 us
    mul x16, other arithmetic, bin_tile(): col_onehot * masked_weight[:, None]  30.8 us
    dot_general x16, matrix products, bin_tile(): lax.dot_general(row_onehot, stacked, (((0,), (0,)), ((), ())), preferred_...  22.6 us
    ppermute x12, starting transfers between devices, extended(): lax.ppermute(lax.slice_in_dim(block, 0, width, axis=dim), axis, backward)  15.5 us
    convert_element_type x16, other arithmetic, bin_tile(): obs_vals.astype(jnp.float32)  14.7 us
  transfers between devices with their start and end apart: 28, of which 22 were waited for; matrix products, arithmetic and copies ran while one was open for 2% of the time, Pallas kernels for 0%

commit v1 on v0

v1 whole, which is shorter than its diff:
```python
import functools

import jax
import jax.numpy as jnp
from jax import lax
from jax.experimental import pallas as pl
from jax.experimental.pallas import tpu as pltpu
from jax.sharding import PartitionSpec as P

TILE = 128
ITERS = 3
HALO = 8
PAD = 2 * HALO
STRIP = 24
CHUNK = 1024

smooth_weight = 0.05

MESH = pl.DeviceIdType.MESH


def greet_all(me, count, cols):
    barrier = pltpu.get_barrier_semaphore()

    def signal(k, carry):
        peer = lax.rem(me + k, count)
        pl.semaphore_signal(
            barrier, inc=1, device_id=(peer // cols, lax.rem(peer, cols)), device_id_type=MESH
        )
        return carry

    lax.fori_loop(1, count, signal, 0)
    pl.semaphore_wait(barrier, count - 1)


def exchange_kernel(rows, cols, code_ref, pair_ref, code_out, pair_out, send_sems, recv_sems, own_sems):
    count = rows * cols
    me = lax.axis_index("row") * cols + lax.axis_index("col")
    own_code = pltpu.make_async_copy(code_ref.at[me], code_out.at[me], own_sems.at[0])
    own_pair = pltpu.make_async_copy(pair_ref.at[me], pair_out.at[me], own_sems.at[1])
    own_code.start()
    own_pair.start()
    greet_all(me, count, cols)

    def copies(k):
        peer = lax.rem(me + k, count)
        where = (peer // cols, lax.rem(peer, cols))
        return [
            pltpu.make_async_remote_copy(
                src_ref=src.at[peer],
                dst_ref=dst.at[me],
                send_sem=send_sems.at[which, k],
                recv_sem=recv_sems.at[which, k],
                device_id=where,
                device_id_type=MESH,
            )
            for which, (src, dst) in enumerate(((code_ref, code_out), (pair_ref, pair_out)))
        ]

    def begin(k, carry):
        for copy in copies(k):
            copy.start()
        return carry

    def finish(k, carry):
        source = lax.rem(me + count - k, count)
        for which, (src, dst) in enumerate(((code_ref, code_out), (pair_ref, pair_out))):
            pltpu.make_async_remote_copy(
                src_ref=src.at[source],
                dst_ref=dst.at[source],
                send_sem=send_sems.at[which, k],
                recv_sem=recv_sems.at[which, k],
                device_id=(source // cols, lax.rem(source, cols)),
                device_id_type=MESH,
            ).wait()
        return carry

    lax.fori_loop(1, count, begin, 0)
    lax.fori_loop(1, count, finish, 0)
    own_code.wait()
    own_pair.wait()


def bin_kernel(members_ref, weight_ref, response_ref):
    slots = members_ref.shape[2]
    chunk = min(CHUNK, slots)
    offsets = (
        lax.broadcasted_iota(jnp.int32, (TILE, chunk), 0).astype(jnp.float32).astype(jnp.bfloat16)
    )
    one = jnp.ones((TILE, chunk), jnp.bfloat16)
    zero = jnp.zeros((TILE, chunk), jnp.bfloat16)

    def part(at, total):
        def spread(which):
            piece = members_ref[0, which : which + 1, pl.ds(pl.multiple_of(at * chunk, chunk), chunk)]
            return jnp.broadcast_to(piece.astype(jnp.bfloat16), (TILE, chunk))

        row_hot = jnp.where(spread(0) == offsets, one, zero)
        col_hit = spread(1) == offsets
        stacked = jnp.concatenate(
            [jnp.where(col_hit, spread(2), zero), jnp.where(col_hit, spread(3), zero)], axis=0
        )
        return total + lax.dot_general(
            row_hot, stacked, (((1,), (1,)), ((), ())), preferred_element_type=jnp.float32
        )

    total = lax.fori_loop(
        0, slots // chunk, part, jnp.zeros((TILE, 2 * TILE), jnp.float32)
    )
    weight_ref[...] = total[:, :TILE]
    response_ref[...] = total[:, TILE:]


def smooth_kernel(
    rows, cols, b_ref, w_ref, k_ref, x_ref, r_ref,
    res, wgt, kap, live, inner, image, along, course,
    send_low, send_high, recv_low, recv_high, mine, sums,
    row_send, row_recv, col_send, col_recv, sum_send, sum_recv,
):
    count = rows * cols
    my_row, my_col = lax.axis_index("row"), lax.axis_index("col")
    me = my_row * cols + my_col
    height, width = b_ref.shape
    full = width + 128
    own = pl.ds(PAD, height)
    fields = ((b_ref, res), (w_ref, wgt), (k_ref, kap))
    tall = res.shape[0]

    for _, field in fields:
        field[0:PAD, :] = jnp.zeros((PAD, full), jnp.float32)
        field[PAD + height :, :] = jnp.zeros((tall - PAD - height, full), jnp.float32)
    inner[0:HALO, :] = jnp.zeros((HALO, full), jnp.float32)
    inner[PAD + height + HALO : 2 * PAD + height, :] = jnp.zeros((HALO, full), jnp.float32)
    recv_low[...] = jnp.zeros_like(recv_low)
    recv_high[...] = jnp.zeros_like(recv_high)
    greet_all(me, count, cols)

    up, down = my_row > 0, my_row < rows - 1
    left, right = my_col > 0, my_col < cols - 1

    def row_copies(way):
        made = []
        for at, (src, dst) in enumerate(fields):
            if way == 0:
                source, target = src.at[pl.ds(0, HALO), :], dst.at[pl.ds(PAD + height, HALO), pl.ds(0, width)]
                where = (my_row - 1, my_col)
            else:
                source, target = src.at[pl.ds(height - HALO, HALO), :], dst.at[pl.ds(HALO, HALO), pl.ds(0, width)]
                where = (my_row + 1, my_col)
            made.append(
                pltpu.make_async_remote_copy(
                    src_ref=source, dst_ref=target,
                    send_sem=row_send.at[way, at], recv_sem=row_recv.at[way, at],
                    device_id=where, device_id_type=MESH,
                )
            )
        return made

    def col_copy(way):
        source, target, where = (
            (send_low, recv_high, (my_row, my_col - 1)),
            (send_high, recv_low, (my_row, my_col + 1)),
        )[way]
        return pltpu.make_async_remote_copy(
            src_ref=source, dst_ref=target, send_sem=col_send.at[way], recv_sem=col_recv.at[way],
            device_id=where, device_id_type=MESH,
        )

    for way, there in ((0, up), (1, down)):

        @pl.when(there)
        def _(way=way):
            for copy in row_copies(way):
                copy.start()

    def fill(i, carry):
        at = pl.multiple_of(i * 32, 32)
        for src, dst in fields:
            dst[pl.ds(PAD + at, 32), 0:width] = src[pl.ds(at, 32), :]
        return carry

    lax.fori_loop(0, height // 32, fill, 0)

    for way, there in ((0, up), (1, down)):

        @pl.when(there)
        def _(way=way):
            for copy in row_copies(way):
                copy.wait_send()

        @pl.when((down, up)[way])
        def _(way=way):
            for copy in row_copies(way):
                copy.wait_recv()

    def pack(i, carry):
        at = pl.multiple_of(i * 128, 128)
        for which, (_, field) in enumerate(fields):
            low = field[pl.ds(at, 128), 0:128].T
            send_low[which * HALO : (which + 1) * HALO, pl.ds(at, 128)] = low[:HALO]
            high = field[pl.ds(at, 128), width - 128 : width].T
            send_high[which * HALO : (which + 1) * HALO, pl.ds(at, 128)] = high[128 - HALO :]
        return carry

    lax.fori_loop(0, tall // 128, pack, 0)
    for way, there in ((0, left), (1, right)):

        @pl.when(there)
        def _(way=way):
            col_copy(way).start()

    for way, there in ((0, left), (1, right)):

        @pl.when(there)
        def _(way=way):
            col_copy(way).wait_send()

        @pl.when((right, left)[way])
        def _(way=way):
            col_copy(way).wait_recv()

    gap = jnp.zeros((128 - 2 * HALO, 128), jnp.float32)

    def unpack(i, carry):
        at = pl.multiple_of(i * 128, 128)
        for which, (_, field) in enumerate(fields):
            part = slice(which * HALO, (which + 1) * HALO)
            both = jnp.concatenate(
                [recv_high[part, pl.ds(at, 128)], gap, recv_low[part, pl.ds(at, 128)]], axis=0
            )
            field[pl.ds(at, 128), width:full] = both.T
        return carry

    lax.fori_loop(0, tall // 128, unpack, 0)

    strips = (height + 2 * HALO) // STRIP
    top = jnp.where(up, HALO, PAD)
    bottom = PAD + height + jnp.where(down, HALO, 0)
    high_end = width + jnp.where(right, HALO, 0)
    low_begin = full - jnp.where(left, HALO, 0)

    def start_of(i):
        return pl.multiple_of(HALO + i * STRIP, 8)

    def prepare(i, carry):
        at = start_of(i)
        row = lax.broadcasted_iota(jnp.int32, (STRIP, full), 0) + at
        col = lax.broadcasted_iota(jnp.int32, (STRIP, full), 1)
        inside = (row >= top) & (row < bottom) & ((col < high_end) | (col >= low_begin))
        mask = jnp.where(inside, 1.0, 0.0).astype(jnp.float32)
        live[pl.ds(at, STRIP), :] = mask
        kap[pl.ds(at, STRIP), :] = jnp.where(inside, 4.0 + kap[pl.ds(at, STRIP), :], 0.0)
        return carry

    lax.fori_loop(0, strips, prepare, 0)

    def stencil(field, at):
        slab = field[pl.ds(pl.multiple_of(at - HALO, 8), STRIP + 2 * HALO), :]
        center = slab[HALO : HALO + STRIP]
        beside = slab[HALO + 1 : HALO + 1 + STRIP] + slab[HALO - 1 : HALO - 1 + STRIP]
        beside = beside + pltpu.roll(center, full - 1, axis=1) + pltpu.roll(center, 1, axis=1)
        here = pl.ds(at, STRIP)
        return kap[here, :] * center - live[here, :] * beside

    def operate():
        def first(i, carry):
            at = start_of(i)
            inner[pl.ds(at, STRIP), :] = stencil(res, at)
            return carry

        def second(i, carry):
            at = start_of(i)
            here = pl.ds(at, STRIP)
            image[here, :] = wgt[here, :] * res[here, :] + smooth_weight * stencil(inner, at)
            return carry

        lax.fori_loop(0, strips, first, 0)
        lax.fori_loop(0, strips, second, 0)

    lane = lax.broadcasted_iota(jnp.int32, (1, 128), 1)

    def two_products(step):
        def add(i, carry):
            norm, curve = carry
            here = pl.ds(pl.multiple_of(PAD + i * 16, 8), 16)
            a, c = res[here, 0:width], image[here, 0:width]
            aa, ac = a * a, a * c
            return norm + (aa[:8] + aa[8:]), curve + (ac[:8] + ac[8:])

        zero = jnp.zeros((8, width), jnp.float32)
        norm, curve = lax.fori_loop(0, height // 16, add, (zero, zero))
        norm = jnp.sum(jnp.sum(norm, axis=0, keepdims=True), axis=1, keepdims=True)
        curve = jnp.sum(jnp.sum(curve, axis=0, keepdims=True), axis=1, keepdims=True)
        both = jnp.where(lane == 0, norm, jnp.where(lane == 1, curve, 0.0))
        mine[step] = both
        sums[step, me] = both

        def copy_to(k, peer, slot):
            return pltpu.make_async_remote_copy(
                src_ref=mine.at[step], dst_ref=sums.at[step, slot],
                send_sem=sum_send.at[step, k], recv_sem=sum_recv.at[step, k],
                device_id=(peer // cols, lax.rem(peer, cols)), device_id_type=MESH,
            )

        def begin(k, carry):
            copy_to(k, lax.rem(me + k, count), me).start()
            return carry

        def finish(k, carry):
            source = lax.rem(me + count - k, count)
            copy_to(k, source, source).wait()
            return carry

        lax.fori_loop(1, count, begin, 0)
        lax.fori_loop(1, count, finish, 0)
        total = jnp.sum(sums[step], axis=0)
        norm = jnp.sum(jnp.where(lane == 0, total, 0.0), axis=1, keepdims=True)
        curve = jnp.sum(jnp.where(lane == 1, total, 0.0), axis=1, keepdims=True)
        return norm, curve

    norm_now = alpha = None
    for step in range(ITERS):
        operate()
        norm_next, curvature = two_products(step)
        if step == 0:
            ratio = None
            alpha = norm_next / curvature
        else:
            ratio = norm_next / norm_now
            alpha = norm_next / (curvature - ratio * norm_next / alpha)
        norm_now = norm_next

        def advance(i, carry, step=step, ratio=ratio, alpha=alpha):
            at = pl.multiple_of(i * 16, 8)
            here = pl.ds(pl.multiple_of(PAD + at, 8), 16)
            mine_rows = pl.ds(at, 16)
            way = res[here, 0:width]
            if step > 0:
                way = way + ratio * course[mine_rows, :]
            if step + 1 < ITERS:
                course[mine_rows, :] = way
            moved = alpha * way
            x_ref[mine_rows, :] = moved if step == 0 else x_ref[mine_rows, :] + moved
            if step + 1 == ITERS:
                r_ref[mine_rows, :] = res[here, 0:width] - alpha * (
                    image[here, 0:width] + ratio * along[here, 0:width]
                )
            return carry

        lax.fori_loop(0, height // 16, advance, 0)

        if step + 1 < ITERS:

            def recede(i, carry, step=step, ratio=ratio, alpha=alpha):
                here = pl.ds(start_of(i), STRIP)
                path = image[here, :]
                if step > 0:
                    path = path + ratio * along[here, :]
                along[here, :] = path
                res[here, :] = res[here, :] - alpha * path
                return carry

            lax.fori_loop(0, strips, recede, 0)


def per_device(rows, cols, obs_cell, obs_value, obs_weight, obs_count, kappa_field):
    count = rows * cols
    height, width = kappa_field.shape
    tiles, _, slots = obs_cell.shape[1:]
    cell = obs_cell[0]
    local = (cell // (width * cols) % TILE) * TILE + cell % TILE
    alive = jnp.arange(slots, dtype=jnp.int32) < obs_count[0][:, :, None]
    code = jnp.where(alive, local, -1).astype(jnp.int16).transpose(1, 0, 2)
    product = (obs_weight[0].astype(jnp.float32) * obs_value[0].astype(jnp.float32)).astype(jnp.bfloat16)
    pair = jnp.concatenate([obs_weight[0].transpose(1, 0, 2), product.transpose(1, 0, 2)], axis=1)

    in_vmem = pl.BlockSpec(memory_space=pltpu.VMEM)
    got_code, got_pair = pl.pallas_call(
        functools.partial(exchange_kernel, rows, cols),
        out_shape=(
            jax.ShapeDtypeStruct(code.shape, code.dtype),
            jax.ShapeDtypeStruct(pair.shape, pair.dtype),
        ),
        in_specs=[in_vmem] * 2,
        out_specs=(in_vmem,) * 2,
        scratch_shapes=[
            pltpu.SemaphoreType.DMA((2, count)),
            pltpu.SemaphoreType.DMA((2, count)),
            pltpu.SemaphoreType.DMA((2,)),
        ],
        compiler_params=pltpu.CompilerParams(collective_id=0, has_side_effects=True),
        name="exchange",
    )(code, pair)

    flat = got_code.astype(jnp.int32).transpose(1, 0, 2).reshape(tiles, 1, count * slots)
    pairs = (
        got_pair.reshape(count, 2, tiles, slots)
        .transpose(2, 1, 0, 3)
        .reshape(tiles, 2, count * slots)
        .astype(jnp.float32)
    )
    members = jnp.concatenate(
        [(flat >> 7).astype(jnp.float32), (flat & (TILE - 1)).astype(jnp.float32), pairs], axis=1
    )
    across = width // TILE
    field = jax.ShapeDtypeStruct((height, width), jnp.float32)
    tile_spec = pl.BlockSpec((TILE, TILE), lambda t: (t // across, t % across))
    weight_field, response = pl.pallas_call(
        bin_kernel,
        grid=(tiles,),
        out_shape=(field, field),
        in_specs=[pl.BlockSpec((1, 4, count * slots), lambda t: (t, 0, 0))],
        out_specs=(tile_spec, tile_spec),
        name="binning",
    )(members)

    full = width + 128
    tall = -(-(height + 2 * PAD) // 128) * 128
    extended = pltpu.VMEM((tall, full), jnp.float32)
    edge = pltpu.VMEM((3 * HALO, tall), jnp.float32)
    return pl.pallas_call(
        functools.partial(smooth_kernel, rows, cols),
        out_shape=(field, field),
        in_specs=[in_vmem] * 3,
        out_specs=(in_vmem,) * 2,
        scratch_shapes=[extended] * 7
        + [pltpu.VMEM((height, width), jnp.float32)]
        + [edge] * 4
        + [
            pltpu.VMEM((ITERS, 1, 128), jnp.float32),
            pltpu.VMEM((ITERS, count, 1, 128), jnp.float32),
            pltpu.SemaphoreType.DMA((2, 3)),
            pltpu.SemaphoreType.DMA((2, 3)),
            pltpu.SemaphoreType.DMA((2,)),
            pltpu.SemaphoreType.DMA((2,)),
            pltpu.SemaphoreType.DMA((ITERS, count)),
            pltpu.SemaphoreType.DMA((ITERS, count)),
        ],
        compiler_params=pltpu.CompilerParams(collective_id=1, has_side_effects=True),
        name="smoothing",
    )(response, weight_field, kappa_field)


def solution(mesh):
    placed = (
        P(("row", "col"), None, None, None),
        P(("row", "col"), None, None, None),
        P(("row", "col"), None, None, None),
        P(("row", "col"), None, None),
        P("row", "col"),
    )
    return jax.shard_map(
        functools.partial(per_device, mesh.shape["row"], mesh.shape["col"]),
        mesh=mesh,
        in_specs=placed,
        out_specs=(P("row", "col"), P("row", "col")),
        check_vma=False,
    )
```

time: 428 us -> 103 us (0.24)
  blocking collectives: 118 us -> 0 us
  waiting for transfers between devices: 109 us -> 0 us
  Pallas kernels: 0 us -> 91 us
  starting transfers between devices: 70.5 us -> 0 us
  other arithmetic: 66.7 us -> 4.62 us
  matrix products: 22.6 us -> 0 us
  local copies, waits for them, and re-layouts: 26.2 us -> 6.26 us
  between operations: 10.6 us -> 0.7 us
    psum x3 -> x0, blocking collectives: 118 us -> none  [two_products(): lax.psum((jnp.sum(current * current), jnp.sum(current * image)), ('row',...]
    pallas_call x0 -> x3, Pallas kernels: none -> 91 us  [the longest x1 49.1 us: per_device(): pl.pallas_call(functools.partial(smooth_kernel, rows, cols), out_shape=(f...]
    ppermute x24 -> x0, waiting for transfers between devices: 82.6 us -> none  [the longest x12 43 us: extended(): lax.ppermute(lax.slice_in_dim(block, block.shape[dim] - width, None, axis...]
    ppermute x24 -> x0, starting transfers between devices: 55.5 us -> none  [the longest x12 40 us: extended(): lax.ppermute(lax.slice_in_dim(block, block.shape[dim] - width, None, axis...]
    mul x16 -> x0, other arithmetic: 30.8 us -> none  [bin_tile(): col_onehot * masked_weight[:, None]]
    all_to_all x4 -> x0, waiting for transfers between devices: 26.3 us -> none  [the longest x1 9.66 us: per_device(): lax.all_to_all(obs_cell, ('row', 'col'), split_axis=2, concat_axis=2, til...]
    dot_general x16 -> x0, matrix products: 22.6 us -> none  [bin_tile(): lax.dot_general(row_onehot, stacked, (((0,), (0,)), ((), ())), preferred_...]
    all_to_all x4 -> x0, starting transfers between devices: 15.1 us -> none  [the longest x1 7.33 us: per_device(): lax.all_to_all(obs_count, ('row', 'col'), split_axis=2, concat_axis=2, ti...]
  transfers between devices with their start and end apart: 28 -> 0, of which waited for: 22 -> 0; matrix products, arithmetic and copies ran while one was open for 2% -> 0% of each run, Pallas kernels for 0% -> 0%
where the time goes in v1:
time: 103 us
  Pallas kernels  91 us (88%)
  local copies, waits for them, and re-layouts  6.26 us (6%)
  other arithmetic  4.62 us (4%)
    pallas_call x1, Pallas kernels, per_device(): pl.pallas_call(functools.partial(smooth_kernel, rows, cols), out_shape=(f...  49.1 us
    pallas_call x1, Pallas kernels, per_device(): pl.pallas_call(bin_kernel, grid=(tiles,), out_shape=(field, field), in_sp...  22.4 us
    pallas_call x1, Pallas kernels, per_device(): pl.pallas_call(functools.partial(exchange_kernel, rows, cols), out_shape=...  19.5 us
    unnamed x11, local copies, waits for them, and re-layouts  4 us
    transpose x1, other arithmetic, per_device(): code = jnp.where(alive, local, -1).astype(jnp.int16).transpose(1, 0, 2)  2.07 us

profile of v1, /device:TPU:0, one launch (start us, length us, event | category | flops | bytes accessed | tf_op | source)
XLA Modules:
  0.0 102.6 jit_solution(3337932955627528524)
XLA Ops:
  0.6 0.8 copy.7
  1.4 0.0 copy-start.1
  1.4 0.0 copy-start.2
  1.4 2.1 %fusion.14.code_ref = s16[32,16,128]{2,1,0:T(8,128)(2,1)} fusion(s32[1,16,32,128]{3,2,1,0:T(8,128)} %param.5, s32[16,32]{0,1:T(8,128)S(1)} %copy.7), kind=kLoop, calls=%fused_computation.32 | loop fusion | flops 2555904 | bytes 395264 | tf_op jit(solution)/shard_map/transpose | solution.py:373
  3.5 0.0 copy-done.1
  3.5 0.0 copy-done.2
  3.5 0.1 fusion.13
  3.6 0.1 copy.22
  3.6 0.7 pad_maximum_fusion.1.pair_ref
  4.4 19.5 %exchange.1 = (s16[32,16,128]{2,1,0:T(8,128)(2,1)}, bf16[32,32,128]{2,1,0:T(8,128)(2,1)}) custom-call(s16[32,16,128]{2,1,0:T(8,128)(2,1)} %fusion.14.code_ref, bf16[32,32,128]{2,1,0:T(8,128)(2,1)} %pad_maximum_fusion.1.pair_ref), custom_call_target="tpu_custom_call" | custom-call | tf_op jit(solution)/shard_map/exchange/pallas_call | solution.py:378
  23.8 1.0 %copy.21 = f32[32,2,16,128]{3,0,1,2:T(8,128)S(1)} copy(bf16[32,2,16,128]{3,2,1,0:T(8,128)(2,1)} %bitcast.57) | data formatting | bytes 786432 | tf_op jit(solution)/shard_map/convert_element_type | solution.py:400
  24.9 0.0 copy-start.3
  24.9 0.3 reshape.53
  25.2 0.6 copy-done.3
  25.8 0.1 fusion.1
  25.9 0.1 copy.11
  25.9 0.1 copy.12
  26.0 1.7 %pad_maximum_fusion.members_ref = f32[16,4,4096]{2,1,0:T(4,128)} fusion(f32[16,2,4096]{2,1,0:T(2,128)S(1)} %reshape.53, f32[16,1,4096]{2,1,0:T(1,128)S(1)} %bitcast.55, f32[16,1,4096]{2,1,0:T(1,128)S(1)} %bitcast.54), kind=kLoop, calls=%fused_computation | loop fusion | flops 524288 | bytes 2097152 | tf_op jit(solution)/shard_map/concatenate | solution.py:402
  27.7 22.4 %binning.1 = (f32[512,512]{1,0:T(8,128)}, f32[512,512]{1,0:T(8,128)}) custom-call(f32[16,4,4096]{2,1,0:T(4,128)} %pad_maximum_fusion.members_ref), custom_call_target="tpu_custom_call" | custom-call | tf_op jit(solution)/shard_map/binning/pallas_call | solution.py:408
  50.1 49.1 %smoothing.1 = (f32[512,512]{1,0:T(8,128)}, f32[512,512]{1,0:T(8,128)}) custom-call(f32[512,512]{1,0:T(8,128)} %get-tuple-element.8.b_ref, f32[512,512]{1,0:T(8,128)} %get-tuple-element.9.w_ref, f32[512,512]{1,0:T(8,128)} %k_ref.1), custom_call_target="tpu_custom_call" | custom-call | tf_op jit(solution)/shard_map/smoothing/pallas_call | solution.py:421
  99.3 0.0 copy-start
  99.3 2.4 %copy.25 = f32[512,512]{1,0:T(8,128)} copy(f32[512,512]{1,0:T(8,128)} %get-tuple-element.14) | data formatting | bytes 2097152
  101.6 0.0 copy-done
  101.6 1.0 copy.26
Async XLA Ops:
  1.4 2.1 %copy-start.1 = (bf16[1,16,32,128]{3,2,1,0:T(8,128)(2,1)S(1)}, bf16[1,16,32,128]{3,2,1,0:T(8,128)(2,1)}, u32[]{:S(2)}) copy-start(bf16[1,16,32,128]{3,2,1,0:T(8,128)(2,1)} %param.7) | copy-start | bytes 393220
  1.4 2.1 %copy-start.2 = (bf16[1,16,32,128]{3,2,1,0:T(8,128)(2,1)S(1)}, bf16[1,16,32,128]{3,2,1,0:T(8,128)(2,1)}, u32[]{:S(2)}) copy-start(bf16[1,16,32,128]{3,2,1,0:T(8,128)(2,1)} %param.6) | copy-start | bytes 393220
  24.9 0.9 copy-start.3
  99.3 2.4 %copy-start = (f32[512,512]{1,0:T(8,128)S(1)}, f32[512,512]{1,0:T(8,128)}, u32[]{:S(2)}) copy-start(f32[512,512]{1,0:T(8,128)} %get-tuple-element.15) | copy-start | bytes 3145732

commit v2 on v1

--- a/solution.py
+++ b/solution.py
@@ -11,8 +11,8 @@
 ITERS = 3
 HALO = 8
 PAD = 2 * HALO
-STRIP = 24
-CHUNK = 1024
+STRIP = 88
+CHUNK = 4096
 
 smooth_weight = 0.05
 
@@ -30,7 +30,10 @@
         return carry
 
     lax.fori_loop(1, count, signal, 0)
-    pl.semaphore_wait(barrier, count - 1)
+
+
+def await_all(count):
+    pl.semaphore_wait(pltpu.get_barrier_semaphore(), count - 1)
 
 
 def exchange_kernel(rows, cols, code_ref, pair_ref, code_out, pair_out, send_sems, recv_sems, own_sems):
@@ -38,9 +41,10 @@
     me = lax.axis_index("row") * cols + lax.axis_index("col")
     own_code = pltpu.make_async_copy(code_ref.at[me], code_out.at[me], own_sems.at[0])
     own_pair = pltpu.make_async_copy(pair_ref.at[me], pair_out.at[me], own_sems.at[1])
+    greet_all(me, count, cols)
     own_code.start()
     own_pair.start()
-    greet_all(me, count, cols)
+    await_all(count)
 
     def copies(k):
         peer = lax.rem(me + k, count)
@@ -95,25 +99,25 @@
             piece = members_ref[0, which : which + 1, pl.ds(pl.multiple_of(at * chunk, chunk), chunk)]
             return jnp.broadcast_to(piece.astype(jnp.bfloat16), (TILE, chunk))
 
-        row_hot = jnp.where(spread(0) == offsets, one, zero)
-        col_hit = spread(1) == offsets
+        col_hot = jnp.where(spread(1) == offsets, one, zero)
+        row_hit = spread(0) == offsets
         stacked = jnp.concatenate(
-            [jnp.where(col_hit, spread(2), zero), jnp.where(col_hit, spread(3), zero)], axis=0
+            [jnp.where(row_hit, spread(2), zero), jnp.where(row_hit, spread(3), zero)], axis=0
         )
         return total + lax.dot_general(
-            row_hot, stacked, (((1,), (1,)), ((), ())), preferred_element_type=jnp.float32
+            stacked, col_hot, (((1,), (1,)), ((), ())), preferred_element_type=jnp.float32
         )
 
     total = lax.fori_loop(
-        0, slots // chunk, part, jnp.zeros((TILE, 2 * TILE), jnp.float32)
-    )
-    weight_ref[...] = total[:, :TILE]
-    response_ref[...] = total[:, TILE:]
+        0, slots // chunk, part, jnp.zeros((2 * TILE, TILE), jnp.float32)
+    )
+    weight_ref[...] = total[:TILE]
+    response_ref[...] = total[TILE:]
 
 
 def smooth_kernel(
     rows, cols, b_ref, w_ref, k_ref, x_ref, r_ref,
-    res, wgt, kap, live, inner, image, along, course,
+    res, wgt, kap, live, inner, image, along, second, further, course,
     send_low, send_high, recv_low, recv_high, mine, sums,
     row_send, row_recv, col_send, col_recv, sum_send, sum_recv,
 ):
@@ -134,6 +138,16 @@
     recv_low[...] = jnp.zeros_like(recv_low)
     recv_high[...] = jnp.zeros_like(recv_high)
     greet_all(me, count, cols)
+
+    def fill(i, carry):
+        at = pl.multiple_of(i * 32, 32)
+        for src, dst in fields:
+            dst[pl.ds(PAD + at, 32), 0:width] = src[pl.ds(at, 32), :]
+        return carry
+
+    lax.fori_loop(0, height // 32, fill, 0)
+
+    await_all(count)
 
     up, down = my_row > 0, my_row < rows - 1
     left, right = my_col > 0, my_col < cols - 1
@@ -173,14 +187,6 @@
             for copy in row_copies(way):
                 copy.start()
 
-    def fill(i, carry):
-        at = pl.multiple_of(i * 32, 32)
-        for src, dst in fields:
-            dst[pl.ds(PAD + at, 32), 0:width] = src[pl.ds(at, 32), :]
-        return carry
-
-    lax.fori_loop(0, height // 32, fill, 0)
-
     for way, there in ((0, up), (1, down)):
 
         @pl.when(there)
@@ -262,66 +268,72 @@
         here = pl.ds(at, STRIP)
         return kap[here, :] * center - live[here, :] * beside
 
-    def operate():
+    def operate(source, target):
         def first(i, carry):
             at = start_of(i)
-            inner[pl.ds(at, STRIP), :] = stencil(res, at)
+            inner[pl.ds(at, STRIP), :] = stencil(source, at)
             return carry
 
-        def second(i, carry):
+        def last(i, carry):
             at = start_of(i)
             here = pl.ds(at, STRIP)
-            image[here, :] = wgt[here, :] * res[here, :] + smooth_weight * stencil(inner, at)
+            target[here, :] = wgt[here, :] * source[here, :] + smooth_weight * stencil(inner, at)
             return carry
 
         lax.fori_loop(0, strips, first, 0)
-        lax.fori_loop(0, strips, second, 0)
+        lax.fori_loop(0, strips, last, 0)
 
     lane = lax.broadcasted_iota(jnp.int32, (1, 128), 1)
 
-    def two_products(step):
+    def copy_to(step, k, peer, slot):
+        return pltpu.make_async_remote_copy(
+            src_ref=mine.at[step], dst_ref=sums.at[step, slot],
+            send_sem=sum_send.at[step, k], recv_sem=sum_recv.at[step, k],
+            device_id=(peer // cols, lax.rem(peer, cols)), device_id_type=MESH,
+        )
+
+    def begin_products(step):
         def add(i, carry):
             norm, curve = carry
-            here = pl.ds(pl.multiple_of(PAD + i * 16, 8), 16)
+            here = pl.ds(pl.multiple_of(PAD + i * 32, 8), 32)
             a, c = res[here, 0:width], image[here, 0:width]
             aa, ac = a * a, a * c
-            return norm + (aa[:8] + aa[8:]), curve + (ac[:8] + ac[8:])
+            norm = norm + ((aa[:8] + aa[8:16]) + (aa[16:24] + aa[24:]))
+            return norm, curve + ((ac[:8] + ac[8:16]) + (ac[16:24] + ac[24:]))
 
         zero = jnp.zeros((8, width), jnp.float32)
-        norm, curve = lax.fori_loop(0, height // 16, add, (zero, zero))
+        norm, curve = lax.fori_loop(0, height // 32, add, (zero, zero))
         norm = jnp.sum(jnp.sum(norm, axis=0, keepdims=True), axis=1, keepdims=True)
         curve = jnp.sum(jnp.sum(curve, axis=0, keepdims=True), axis=1, keepdims=True)
         both = jnp.where(lane == 0, norm, jnp.where(lane == 1, curve, 0.0))
         mine[step] = both
         sums[step, me] = both
 
-        def copy_to(k, peer, slot):
-            return pltpu.make_async_remote_copy(
-                src_ref=mine.at[step], dst_ref=sums.at[step, slot],
-                send_sem=sum_send.at[step, k], recv_sem=sum_recv.at[step, k],
-                device_id=(peer // cols, lax.rem(peer, cols)), device_id_type=MESH,
-            )
-
         def begin(k, carry):
-            copy_to(k, lax.rem(me + k, count), me).start()
+            copy_to(step, k, lax.rem(me + k, count), me).start()
             return carry
 
+        lax.fori_loop(1, count, begin, 0)
+
+    def end_products(step):
         def finish(k, carry):
             source = lax.rem(me + count - k, count)
-            copy_to(k, source, source).wait()
+            copy_to(step, k, source, source).wait()
             return carry
 
-        lax.fori_loop(1, count, begin, 0)
         lax.fori_loop(1, count, finish, 0)
         total = jnp.sum(sums[step], axis=0)
         norm = jnp.sum(jnp.where(lane == 0, total, 0.0), axis=1, keepdims=True)
         curve = jnp.sum(jnp.where(lane == 1, total, 0.0), axis=1, keepdims=True)
         return norm, curve
 
+    operate(res, image)
+    begin_products(0)
     norm_now = alpha = None
     for step in range(ITERS):
-        operate()
-        norm_next, curvature = two_products(step)
+        if step + 1 < ITERS:
+            operate(image, second)
+        norm_next, curvature = end_products(step)
         if step == 0:
             ratio = None
             alpha = norm_next / curvature
@@ -330,37 +342,41 @@
             alpha = norm_next / (curvature - ratio * norm_next / alpha)
         norm_now = norm_next
 
+        if step + 1 < ITERS:
+
+            def recede(i, carry, step=step, ratio=ratio, alpha=alpha):
+                here = pl.ds(pl.multiple_of(HALO + i * 24, 8), 24)
+                way, path, next_path = res[here, :], image[here, :], second[here, :]
+                old, old_image = way, path
+                if step > 0:
+                    way = way + ratio * course[here, :]
+                    path = path + ratio * along[here, :]
+                    next_path = next_path + ratio * further[here, :]
+                course[here, :] = way
+                along[here, :] = path
+                further[here, :] = next_path
+                res[here, :] = old - alpha * path
+                image[here, :] = old_image - alpha * next_path
+                return carry
+
+            lax.fori_loop(0, (height + 2 * HALO) // 24, recede, 0)
+            begin_products(step + 1)
+
         def advance(i, carry, step=step, ratio=ratio, alpha=alpha):
-            at = pl.multiple_of(i * 16, 8)
-            here = pl.ds(pl.multiple_of(PAD + at, 8), 16)
-            mine_rows = pl.ds(at, 16)
-            way = res[here, 0:width]
-            if step > 0:
-                way = way + ratio * course[mine_rows, :]
+            at = pl.multiple_of(i * 32, 32)
+            here = pl.ds(pl.multiple_of(PAD + at, 8), 32)
+            rows_here = pl.ds(at, 32)
             if step + 1 < ITERS:
-                course[mine_rows, :] = way
-            moved = alpha * way
-            x_ref[mine_rows, :] = moved if step == 0 else x_ref[mine_rows, :] + moved
-            if step + 1 == ITERS:
-                r_ref[mine_rows, :] = res[here, 0:width] - alpha * (
+                moved = alpha * course[here, 0:width]
+            else:
+                moved = alpha * (res[here, 0:width] + ratio * course[here, 0:width])
+                r_ref[rows_here, :] = res[here, 0:width] - alpha * (
                     image[here, 0:width] + ratio * along[here, 0:width]
                 )
+            x_ref[rows_here, :] = moved if step == 0 else x_ref[rows_here, :] + moved
             return carry
 
-        lax.fori_loop(0, height // 16, advance, 0)
-
-        if step + 1 < ITERS:
-
-            def recede(i, carry, step=step, ratio=ratio, alpha=alpha):
-                here = pl.ds(start_of(i), STRIP)
-                path = image[here, :]
-                if step > 0:
-                    path = path + ratio * along[here, :]
-                along[here, :] = path
-                res[here, :] = res[here, :] - alpha * path
-                return carry
-
-            lax.fori_loop(0, strips, recede, 0)
+        lax.fori_loop(0, height // 32, advance, 0)
 
 
 def per_device(rows, cols, obs_cell, obs_value, obs_weight, obs_count, kappa_field):
@@ -388,7 +404,7 @@
             pltpu.SemaphoreType.DMA((2, count)),
             pltpu.SemaphoreType.DMA((2,)),
         ],
-        compiler_params=pltpu.CompilerParams(collective_id=0, has_side_effects=True),
+        compiler_params=pltpu.CompilerParams(collective_id=0, has_side_effects=True, vmem_limit_bytes=8 << 20),
         name="exchange",
     )(code, pair)
 
@@ -411,6 +427,7 @@
         out_shape=(field, field),
         in_specs=[pl.BlockSpec((1, 4, count * slots), lambda t: (t, 0, 0))],
         out_specs=(tile_spec, tile_spec),
+        compiler_params=pltpu.CompilerParams(vmem_limit_bytes=24 << 20),
         name="binning",
     )(members)
 
@@ -423,8 +440,7 @@
         out_shape=(field, field),
         in_specs=[in_vmem] * 3,
         out_specs=(in_vmem,) * 2,
-        scratch_shapes=[extended] * 7
-        + [pltpu.VMEM((height, width), jnp.float32)]
+        scratch_shapes=[extended] * 10
         + [edge] * 4
         + [
             pltpu.VMEM((ITERS, 1, 128), jnp.float32),
@@ -436,7 +452,7 @@
             pltpu.SemaphoreType.DMA((ITERS, count)),
             pltpu.SemaphoreType.DMA((ITERS, count)),
         ],
-        compiler_params=pltpu.CompilerParams(collective_id=1, has_side_effects=True),
+        compiler_params=pltpu.CompilerParams(collective_id=1, has_side_effects=True, vmem_limit_bytes=32 << 20),
         name="smoothing",
     )(response, weight_field, kappa_field)
 

time: 103 us -> 69.9 us (0.68)
  Pallas kernels: 91 us -> 63.3 us
  local copies, waits for them, and re-layouts: 6.26 us -> 3.32 us
  other arithmetic: 4.62 us -> 2.3 us
    pallas_call x1, Pallas kernels: 49.1 us -> 33.3 us  [per_device(): pl.pallas_call(functools.partial(smooth_kernel, rows, cols), out_shape=(f...]
    pallas_call x1, Pallas kernels: 22.4 us -> 12 us  [per_device(): pl.pallas_call(bin_kernel, grid=(tiles,), out_shape=(field, field), in_sp...]
    unnamed x11 -> x9, local copies, waits for them, and re-layouts: 4 us -> 2.01 us
    pallas_call x1, Pallas kernels: 19.5 us -> 18 us  [per_device(): pl.pallas_call(functools.partial(exchange_kernel, rows, cols), out_shape=...]
where the time goes in v2:
time: 69.9 us; the launch traced here: 69.7 us
  Pallas kernels  63.3 us (91%)
  local copies, waits for them, and re-layouts  3.32 us (5%)
  other arithmetic  2.3 us (3%)
  between operations  0.75 us (1%)
    pallas_call x1, Pallas kernels, per_device(): pl.pallas_call(functools.partial(smooth_kernel, rows, cols), out_shape=(f...  33.3 us
    pallas_call x1, Pallas kernels, per_device(): pl.pallas_call(functools.partial(exchange_kernel, rows, cols), out_shape=...  18 us
    pallas_call x1, Pallas kernels, per_device(): pl.pallas_call(bin_kernel, grid=(tiles,), out_shape=(field, field), in_sp...  12 us
    unnamed x9, local copies, waits for them, and re-layouts  2.01 us
    transpose x1, other arithmetic, per_device(): code = jnp.where(alive, local, -1).astype(jnp.int16).transpose(1, 0, 2)  1.42 us

profile of v2, /device:TPU:0, one launch (start us, length us, event | category | flops | bytes accessed | tf_op | source)
XLA Modules:
  0.0 69.7 jit_solution(8453044364776176102)
XLA Ops:
  0.6 0.8 %copy.7 = s32[16,32]{0,1:T(8,128)S(1)} copy(s32[16,32]{1,0:T(8,128)} %bitcast.58) | data formatting | bytes 4096 | tf_op jit(solution)/shard_map/lt | solution.py:388
  1.4 0.0 copy-start.1
  1.4 0.0 copy-start.2
  1.4 1.4 %fusion.14.code_ref = s16[32,16,128]{2,1,0:T(8,128)(2,1)S(1)} fusion(s32[1,16,32,128]{3,2,1,0:T(8,128)} %param.5, s32[16,32]{0,1:T(8,128)S(1)} %copy.7), kind=kLoop, calls=%fused_computation.32 | loop fusion | flops 2555904 | bytes 395264 | tf_op jit(solution)/shard_map/transpose | solution.py:389
  2.8 0.0 copy-done.1
  2.8 0.0 copy-done.2
  2.8 0.1 fusion.13
  2.9 0.1 copy.22
  3.0 18.0 %exchange.1 = (s16[32,16,128]{2,1,0:T(8,128)(2,1)S(1)}, bf16[32,32,128]{2,1,0:T(8,128)(2,1)S(1)}) custom-call(s16[32,16,128]{2,1,0:T(8,128)(2,1)S(1)} %fusion.14.code_ref, bf16[32,32,128]{2,1,0:T(8,128)(2,1)S(1)} %pad_maximum_fusion.1.pair_ref), custom_call_target="tpu_custom_call" | custom-call | tf_op jit(solution)/shard_map/exchange/pallas_call | solution.py:394
  21.0 0.1 copy.21
  21.1 0.3 reshape.53
  21.4 0.1 fusion.1
  21.5 0.1 copy.11
  21.6 0.1 copy.12
  21.6 0.7 %pad_maximum_fusion.members_ref = f32[16,4,4096]{2,1,0:T(4,128)S(1)} fusion(f32[16,2,4096]{2,1,0:T(2,128)S(1)} %reshape.53, f32[16,1,4096]{2,1,0:T(1,128)S(1)} %bitcast.56, f32[16,1,4096]{2,1,0:T(1,128)S(1)} %bitcast.55), kind=kLoop, calls=%fused_computation | loop fusion | flops 524288 | bytes 2097152 | tf_op jit(solution)/shard_map/concatenate | solution.py:418
  22.4 0.0 copy-start
  22.4 12.0 %binning.1 = (f32[512,512]{1,0:T(8,128)S(1)}, f32[512,512]{1,0:T(8,128)S(1)}) custom-call(f32[16,4,4096]{2,1,0:T(4,128)S(1)} %pad_maximum_fusion.members_ref), custom_call_target="tpu_custom_call" | custom-call | tf_op jit(solution)/shard_map/binning/pallas_call | solution.py:424
  34.4 0.0 copy-done
  34.4 33.3 %smoothing.1 = (f32[512,512]{1,0:T(8,128)S(1)}, f32[512,512]{1,0:T(8,128)S(1)}) custom-call(f32[512,512]{1,0:T(8,128)S(1)} %get-tuple-element.8.b_ref, f32[512,512]{1,0:T(8,128)S(1)} %get-tuple-element.9.w_ref, f32[512,512]{1,0:T(8,128)S(1)} %copy-done), custom_call_target="tpu_custom_call" | custom-call | tf_op jit(solution)/shard_map/smoothing/pallas_call | solution.py:438
  67.7 1.0 %copy.25 = f32[512,512]{1,0:T(8,128)} copy(f32[512,512]{1,0:T(8,128)S(1)} %get-tuple-element.14) | data formatting | bytes 2097152
  68.7 1.0 %copy.26 = f32[512,512]{1,0:T(8,128)} copy(f32[512,512]{1,0:T(8,128)S(1)} %get-tuple-element.15) | data formatting | bytes 2097152
  (1 shorter events, 0.0 us)
Async XLA Ops:
  1.4 1.4 %copy-start.1 = (bf16[1,16,32,128]{3,2,1,0:T(8,128)(2,1)S(1)}, bf16[1,16,32,128]{3,2,1,0:T(8,128)(2,1)}, u32[]{:S(2)}) copy-start(bf16[1,16,32,128]{3,2,1,0:T(8,128)(2,1)} %param.7) | copy-start | bytes 393220
  1.4 1.4 %copy-start.2 = (bf16[1,16,32,128]{3,2,1,0:T(8,128)(2,1)S(1)}, bf16[1,16,32,128]{3,2,1,0:T(8,128)(2,1)}, u32[]{:S(2)}) copy-start(bf16[1,16,32,128]{3,2,1,0:T(8,128)(2,1)} %param.6) | copy-start | bytes 393220
  22.4 12.1 %copy-start = (f32[512,512]{1,0:T(8,128)S(1)}, f32[512,512]{1,0:T(8,128)}, u32[]{:S(2)}) copy-start(f32[512,512]{1,0:T(8,128)} %k_ref.1) | copy-start | bytes 3145732

commit v3 on v2

--- a/solution.py
+++ b/solution.py
@@ -11,8 +11,9 @@
 ITERS = 3
 HALO = 8
 PAD = 2 * HALO
-STRIP = 88
-CHUNK = 4096
+STRIP = 176
+SOURCES = 32
+GROUP = 8
 
 smooth_weight = 0.05
 
@@ -36,83 +37,106 @@
     pl.semaphore_wait(pltpu.get_barrier_semaphore(), count - 1)
 
 
-def exchange_kernel(rows, cols, code_ref, pair_ref, code_out, pair_out, send_sems, recv_sems, own_sems):
-    count = rows * cols
+def observe_kernel(
+    rows, cols, code_ref, pair_ref, weight_ref, response_ref,
+    code_in, pair_in, place_row, place_col, amounts, send_sems, recv_sems, own_sems,
+):
+    count, groups, each, slots = code_ref.shape
     me = lax.axis_index("row") * cols + lax.axis_index("col")
-    own_code = pltpu.make_async_copy(code_ref.at[me], code_out.at[me], own_sems.at[0])
-    own_pair = pltpu.make_async_copy(pair_ref.at[me], pair_out.at[me], own_sems.at[1])
+    own_code = pltpu.make_async_copy(code_ref.at[me], code_in.at[me], own_sems.at[0])
+    own_pair = pltpu.make_async_copy(pair_ref.at[me], pair_in.at[me], own_sems.at[1])
     greet_all(me, count, cols)
     own_code.start()
     own_pair.start()
     await_all(count)
-
-    def copies(k):
-        peer = lax.rem(me + k, count)
-        where = (peer // cols, lax.rem(peer, cols))
+    buffers = ((code_ref, code_in), (pair_ref, pair_in))
+
+    def copies(group, k, peer, slot):
         return [
             pltpu.make_async_remote_copy(
-                src_ref=src.at[peer],
-                dst_ref=dst.at[me],
-                send_sem=send_sems.at[which, k],
-                recv_sem=recv_sems.at[which, k],
-                device_id=where,
+                src_ref=src.at[peer, group],
+                dst_ref=dst.at[slot, group],
+                send_sem=send_sems.at[group, which, k],
+                recv_sem=recv_sems.at[group, which, k],
+                device_id=(peer // cols, lax.rem(peer, cols)),
                 device_id_type=MESH,
             )
-            for which, (src, dst) in enumerate(((code_ref, code_out), (pair_ref, pair_out)))
+            for which, (src, dst) in enumerate(buffers)
         ]
 
-    def begin(k, carry):
-        for copy in copies(k):
-            copy.start()
-        return carry
-
-    def finish(k, carry):
-        source = lax.rem(me + count - k, count)
-        for which, (src, dst) in enumerate(((code_ref, code_out), (pair_ref, pair_out))):
-            pltpu.make_async_remote_copy(
-                src_ref=src.at[source],
-                dst_ref=dst.at[source],
-                send_sem=send_sems.at[which, k],
-                recv_sem=recv_sems.at[which, k],
-                device_id=(source // cols, lax.rem(source, cols)),
-                device_id_type=MESH,
-            ).wait()
-        return carry
-
-    lax.fori_loop(1, count, begin, 0)
-    lax.fori_loop(1, count, finish, 0)
+    for group in range(groups):
+
+        def begin(k, carry, group=group):
+            for copy in copies(group, k, lax.rem(me + k, count), me):
+                copy.start()
+            return carry
+
+        lax.fori_loop(1, count, begin, 0)
     own_code.wait()
     own_pair.wait()
 
-
-def bin_kernel(members_ref, weight_ref, response_ref):
-    slots = members_ref.shape[2]
-    chunk = min(CHUNK, slots)
+    bunch = min(SOURCES, count)
+    chunk = bunch * slots
     offsets = (
         lax.broadcasted_iota(jnp.int32, (TILE, chunk), 0).astype(jnp.float32).astype(jnp.bfloat16)
     )
     one = jnp.ones((TILE, chunk), jnp.bfloat16)
     zero = jnp.zeros((TILE, chunk), jnp.bfloat16)
-
-    def part(at, total):
-        def spread(which):
-            piece = members_ref[0, which : which + 1, pl.ds(pl.multiple_of(at * chunk, chunk), chunk)]
-            return jnp.broadcast_to(piece.astype(jnp.bfloat16), (TILE, chunk))
-
-        col_hot = jnp.where(spread(1) == offsets, one, zero)
-        row_hit = spread(0) == offsets
-        stacked = jnp.concatenate(
-            [jnp.where(row_hit, spread(2), zero), jnp.where(row_hit, spread(3), zero)], axis=0
-        )
-        return total + lax.dot_general(
-            stacked, col_hot, (((1,), (1,)), ((), ())), preferred_element_type=jnp.float32
-        )
-
-    total = lax.fori_loop(
-        0, slots // chunk, part, jnp.zeros((2 * TILE, TILE), jnp.float32)
-    )
-    weight_ref[...] = total[:TILE]
-    response_ref[...] = total[TILE:]
+    across = weight_ref.shape[1] // TILE
+
+    for group in range(groups):
+
+        def finish(k, carry, group=group):
+            source = lax.rem(me + count - k, count)
+            for copy in copies(group, k, source, source):
+                copy.wait()
+            return carry
+
+        lax.fori_loop(1, count, finish, 0)
+
+        def decode(i, carry, group=group):
+            some = pl.ds(i * 8, 8)
+            code = code_in[some, group].astype(jnp.int32).reshape(8 * each, slots)
+            here = pl.ds(pl.multiple_of(i * 8 * each, 8 * each), 8 * each)
+            place_row[here, :] = (code >> 7).astype(jnp.float32)
+            place_col[here, :] = (code & (TILE - 1)).astype(jnp.float32)
+            pair = pair_in[some, group].astype(jnp.float32).reshape(16 * each, slots)
+            amounts[pl.ds(pl.multiple_of(i * 16 * each, 16 * each), 16 * each), :] = pair
+            return carry
+
+        lax.fori_loop(0, count // 8, decode, 0, unroll=2)
+
+        def bin_tile(at, carry, group=group):
+            def part(i, total):
+                def spread(ref, first, step):
+                    piece = ref[pl.ds(i * (bunch * step) + first, bunch, stride=step), :]
+                    line = jnp.concatenate([piece[n : n + 1] for n in range(bunch)], axis=1)
+                    return jnp.broadcast_to(line.astype(jnp.bfloat16), (TILE, chunk))
+
+                col_hot = jnp.where(spread(place_col, at, each) == offsets, one, zero)
+                row_hit = spread(place_row, at, each) == offsets
+                weight = spread(amounts, at, 2 * each)
+                product = spread(amounts, at + each, 2 * each)
+                stacked = jnp.concatenate(
+                    [jnp.where(row_hit, weight, zero), jnp.where(row_hit, product, zero)], axis=0
+                )
+                return total + lax.dot_general(
+                    stacked, col_hot, (((1,), (1,)), ((), ())), preferred_element_type=jnp.float32
+                )
+
+            total = lax.fori_loop(
+                0, count // bunch, part, jnp.zeros((2 * TILE, TILE), jnp.float32)
+            )
+            tile = group * each + at
+            where = (
+                pl.ds(pl.multiple_of((tile // across) * TILE, TILE), TILE),
+                pl.ds(pl.multiple_of((tile % across) * TILE, TILE), TILE),
+            )
+            weight_ref[where] = total[:TILE]
+            response_ref[where] = total[TILE:]
+            return carry
+
+        lax.fori_loop(0, each, bin_tile, 0, unroll=4)
 
 
 def smooth_kernel(
@@ -208,7 +232,7 @@
             send_high[which * HALO : (which + 1) * HALO, pl.ds(at, 128)] = high[128 - HALO :]
         return carry
 
-    lax.fori_loop(0, tall // 128, pack, 0)
+    lax.fori_loop(0, tall // 128, pack, 0, unroll=True)
     for way, there in ((0, left), (1, right)):
 
         @pl.when(there)
@@ -237,7 +261,7 @@
             field[pl.ds(at, 128), width:full] = both.T
         return carry
 
-    lax.fori_loop(0, tall // 128, unpack, 0)
+    lax.fori_loop(0, tall // 128, unpack, 0, unroll=True)
 
     strips = (height + 2 * HALO) // STRIP
     top = jnp.where(up, HALO, PAD)
@@ -313,7 +337,7 @@
             copy_to(step, k, lax.rem(me + k, count), me).start()
             return carry
 
-        lax.fori_loop(1, count, begin, 0)
+        lax.fori_loop(1, count, begin, 0, unroll=True)
 
     def end_products(step):
         def finish(k, carry):
@@ -321,7 +345,7 @@
             copy_to(step, k, source, source).wait()
             return carry
 
-        lax.fori_loop(1, count, finish, 0)
+        lax.fori_loop(1, count, finish, 0, unroll=True)
         total = jnp.sum(sums[step], axis=0)
         norm = jnp.sum(jnp.where(lane == 0, total, 0.0), axis=1, keepdims=True)
         curve = jnp.sum(jnp.where(lane == 1, total, 0.0), axis=1, keepdims=True)
@@ -345,7 +369,7 @@
         if step + 1 < ITERS:
 
             def recede(i, carry, step=step, ratio=ratio, alpha=alpha):
-                here = pl.ds(pl.multiple_of(HALO + i * 24, 8), 24)
+                here = pl.ds(pl.multiple_of(HALO + i * 48, 8), 48)
                 way, path, next_path = res[here, :], image[here, :], second[here, :]
                 old, old_image = way, path
                 if step > 0:
@@ -359,7 +383,7 @@
                 image[here, :] = old_image - alpha * next_path
                 return carry
 
-            lax.fori_loop(0, (height + 2 * HALO) // 24, recede, 0)
+            lax.fori_loop(0, (height + 2 * HALO) // 48, recede, 0)
             begin_products(step + 1)
 
         def advance(i, carry, step=step, ratio=ratio, alpha=alpha):
@@ -388,48 +412,38 @@
     alive = jnp.arange(slots, dtype=jnp.int32) < obs_count[0][:, :, None]
     code = jnp.where(alive, local, -1).astype(jnp.int16).transpose(1, 0, 2)
     product = (obs_weight[0].astype(jnp.float32) * obs_value[0].astype(jnp.float32)).astype(jnp.bfloat16)
-    pair = jnp.concatenate([obs_weight[0].transpose(1, 0, 2), product.transpose(1, 0, 2)], axis=1)
+    groups = tiles // GROUP
+    code = code.reshape(count, groups, GROUP, slots)
+    pair = jnp.concatenate(
+        [
+            array.transpose(1, 0, 2).reshape(count, groups, GROUP, slots)
+            for array in (obs_weight[0], product)
+        ],
+        axis=2,
+    )
 
     in_vmem = pl.BlockSpec(memory_space=pltpu.VMEM)
-    got_code, got_pair = pl.pallas_call(
-        functools.partial(exchange_kernel, rows, cols),
-        out_shape=(
-            jax.ShapeDtypeStruct(code.shape, code.dtype),
-            jax.ShapeDtypeStruct(pair.shape, pair.dtype),
-        ),
+    field = jax.ShapeDtypeStruct((height, width), jnp.float32)
+    weight_field, response = pl.pallas_call(
+        functools.partial(observe_kernel, rows, cols),
+        out_shape=(field, field),
         in_specs=[in_vmem] * 2,
         out_specs=(in_vmem,) * 2,
         scratch_shapes=[
-            pltpu.SemaphoreType.DMA((2, count)),
-            pltpu.SemaphoreType.DMA((2, count)),
+            pltpu.VMEM(code.shape, code.dtype),
+            pltpu.VMEM(pair.shape, pair.dtype),
+            pltpu.VMEM((count * GROUP, slots), jnp.float32),
+            pltpu.VMEM((count * GROUP, slots), jnp.float32),
+            pltpu.VMEM((count * GROUP * 2, slots), jnp.float32),
+            pltpu.SemaphoreType.DMA((groups, 2, count)),
+            pltpu.SemaphoreType.DMA((groups, 2, count)),
             pltpu.SemaphoreType.DMA((2,)),
         ],
-        compiler_params=pltpu.CompilerParams(collective_id=0, has_side_effects=True, vmem_limit_bytes=8 << 20),
-        name="exchange",
+        compiler_params=pltpu.CompilerParams(
+            collective_id=0, has_side_effects=True, vmem_limit_bytes=32 << 20
+        ),
+        name="observe",
     )(code, pair)
-
-    flat = got_code.astype(jnp.int32).transpose(1, 0, 2).reshape(tiles, 1, count * slots)
-    pairs = (
-        got_pair.reshape(count, 2, tiles, slots)
-        .transpose(2, 1, 0, 3)
-        .reshape(tiles, 2, count * slots)
-        .astype(jnp.float32)
-    )
-    members = jnp.concatenate(
-        [(flat >> 7).astype(jnp.float32), (flat & (TILE - 1)).astype(jnp.float32), pairs], axis=1
-    )
-    across = width // TILE
-    field = jax.ShapeDtypeStruct((height, width), jnp.float32)
-    tile_spec = pl.BlockSpec((TILE, TILE), lambda t: (t // across, t % across))
-    weight_field, response = pl.pallas_call(
-        bin_kernel,
-        grid=(tiles,),
-        out_shape=(field, field),
-        in_specs=[pl.BlockSpec((1, 4, count * slots), lambda t: (t, 0, 0))],
-        out_specs=(tile_spec, tile_spec),
-        compiler_params=pltpu.CompilerParams(vmem_limit_bytes=24 << 20),
-        name="binning",
-    )(members)
 
     full = width + 128
     tall = -(-(height + 2 * PAD) // 128) * 128

time: 69.9 us -> 63.1 us (0.903)
  Pallas kernels: 63.3 us -> 58.7 us
  local copies, waits for them, and re-layouts: 3.32 us -> 2.12 us
  other arithmetic: 2.3 us -> 1.44 us
    pallas_call x2 -> x1, Pallas kernels: 30 us -> 26.9 us  [per_device(): pl.pallas_call(functools.partial(observe_kernel, rows, cols), out_shape=(...]
    pallas_call x1, Pallas kernels: 33.3 us -> 31.8 us  [per_device(): pl.pallas_call(functools.partial(smooth_kernel, rows, cols), out_shape=(f...]
    lt x1 -> x0, local copies, waits for them, and re-layouts: 0.77 us -> none  [per_device(): alive = jnp.arange(slots, dtype=jnp.int32) < obs_count[0][:, :, None]]
    unnamed x9 -> x8, local copies, waits for them, and re-layouts: 2.01 us -> 1.96 us
where the time goes in v3:
time: 63.1 us; the launch traced here: 63 us
  Pallas kernels  58.7 us (93%)
  local copies, waits for them, and re-layouts  2.12 us (3%)
  other arithmetic  1.44 us (2%)
  between operations  0.72 us (1%)
    pallas_call x1, Pallas kernels, per_device(): pl.pallas_call(functools.partial(smooth_kernel, rows, cols), out_shape=(f...  31.8 us
    pallas_call x1, Pallas kernels, per_device(): pl.pallas_call(functools.partial(observe_kernel, rows, cols), out_shape=(...  26.9 us
    unnamed x8, local copies, waits for them, and re-layouts  1.96 us
    transpose x1, other arithmetic, per_device(): code = jnp.where(alive, local, -1).astype(jnp.int16).transpose(1, 0, 2)  1.35 us

profile of v3, /device:TPU:0, one launch (start us, length us, event | category | flops | bytes accessed | tf_op | source)
XLA Modules:
  0.0 63.0 jit_solution(686348896078004275)
XLA Ops:
  0.6 0.0 copy-start.1
  0.6 0.0 copy-start.2
  0.7 1.4 %fusion.10 = s16[32,16,128]{2,0,1:T(8,128)(2,1)S(1)} fusion(s32[1,16,32,128]{3,2,1,0:T(8,128)} %param.5, s32[16,32]{1,0:T(8,128)} %bitcast.47), kind=kLoop, calls=%fused_computation.27 | loop fusion | flops 2555904 | bytes 395264 | tf_op jit(solution)/shard_map/transpose | solution.py:413
  2.0 0.0 copy-start
  2.0 0.1 copy.13
  2.1 0.0 copy-done.1
  2.1 0.0 copy-done.2
  2.1 0.1 copy_bitcast_fusion
  2.3 26.9 %observe.1 = (f32[512,512]{1,0:T(8,128)S(1)}, f32[512,512]{1,0:T(8,128)S(1)}) custom-call(s16[32,2,8,128]{3,2,1,0:T(8,128)(2,1)S(1)} %bitcast.45, bf16[32,2,16,128]{3,2,1,0:T(8,128)(2,1)S(1)} %pad_maximum_fusion.pair_ref), custom_call_target="tpu_custom_call" | custom-call | tf_op jit(solution)/shard_map/observe/pallas_call | solution.py:427
  29.2 0.0 copy-done
  29.2 31.8 %smoothing.1 = (f32[512,512]{1,0:T(8,128)S(1)}, f32[512,512]{1,0:T(8,128)S(1)}) custom-call(f32[512,512]{1,0:T(8,128)S(1)} %get-tuple-element.4.b_ref, f32[512,512]{1,0:T(8,128)S(1)} %get-tuple-element.5.w_ref, f32[512,512]{1,0:T(8,128)S(1)} %copy-done), custom_call_target="tpu_custom_call" | custom-call | tf_op jit(solution)/shard_map/smoothing/pallas_call | solution.py:452
  61.0 1.0 %copy.16 = f32[512,512]{1,0:T(8,128)} copy(f32[512,512]{1,0:T(8,128)S(1)} %get-tuple-element.10) | data formatting | bytes 2097152
  62.0 1.0 %copy.17 = f32[512,512]{1,0:T(8,128)} copy(f32[512,512]{1,0:T(8,128)S(1)} %get-tuple-element.11) | data formatting | bytes 2097152
  (2 shorter events, 0.1 us)
Async XLA Ops:
  0.6 1.4 %copy-start.1 = (bf16[1,16,32,128]{3,2,1,0:T(8,128)(2,1)S(1)}, bf16[1,16,32,128]{3,2,1,0:T(8,128)(2,1)}, u32[]{:S(2)}) copy-start(bf16[1,16,32,128]{3,2,1,0:T(8,128)(2,1)} %param.7) | copy-start | bytes 393220
  0.6 1.4 %copy-start.2 = (bf16[1,16,32,128]{3,2,1,0:T(8,128)(2,1)S(1)}, bf16[1,16,32,128]{3,2,1,0:T(8,128)(2,1)}, u32[]{:S(2)}) copy-start(bf16[1,16,32,128]{3,2,1,0:T(8,128)(2,1)} %param.6) | copy-start | bytes 393220
  2.0 27.2 %copy-start = (f32[512,512]{1,0:T(8,128)S(1)}, f32[512,512]{1,0:T(8,128)}, u32[]{:S(2)}) copy-start(f32[512,512]{1,0:T(8,128)} %k_ref.1) | copy-start | bytes 3145732
